TPU v7x, 32 devices: a whole 2x2x4 slice. The times are simulated.
32 devices in a mesh: row: 8 (over z, core), col: 4 (over y, x).
Axes of the slice: x: 2, y: 2, z: 4, core: 2. Of those that a mesh axis runs over, the one named last changes fastest.
Arguments:
- u_start: float32 [128, 131072], P('col', 'row'), may hold values from -24 to 24
- v_start: float32 [128, 65536], P('row', 'col'), may hold values from -24 to 24
- keep_u: float32 [128, 40], replicated, may hold values from -1 to 1, as said below
- keep_v: float32 [128, 40], replicated, may hold values from -1 to 1, as said below
- v_next: float32 [65536], P(('col', 'row')), may hold values from -96 to 96
- tile_blocks: bfloat16 [2048, 256, 256], P(('row', 'col')), may hold values from -0.375 to 0.375
- tile_rows: int32 [2048], P(('row', 'col')), may hold values from 0 to 63
- tile_cols: int32 [2048], P(('row', 'col')), may hold values from 0 to 63
- tile_count: int32 [32], P(('row', 'col')), may hold values from 32 to 64
Outputs:
- u_basis: float32 [42, 131072], P(None, ('row', 'col'))
- v_basis: float32 [43, 65536], P(None, ('col', 'row'))
- bidiagonal: float32 [2, 2], replicated
Inputs may be any that keep to these rules, and one draw needn't show every extreme that they name: `tile_rows`: tile row within the device's row group. `tile_cols`: tile column within the device's column group. `tile_count`: slots at this index and beyond hold no tile. `keep_u`: the columns are orthonormal. `keep_v`: the columns are orthonormal.
All inputs are finite; a program needn't handle non-finite values.
Results may differ from a plain program's by a relative error of at most 0.00155.
Values may be sent and summed in bfloat16 or wider, within the bound.
A program may use at most 64 MiB of HBM per device.

v0:
```python
import jax
import jax.numpy as jnp
from jax import lax
from jax.sharding import PartitionSpec as P

STEPS = 2


HIGH = lax.Precision.HIGHEST


def orthonormal(basis_rows, vector, length, gram_matrix):
    first_coef = lax.psum(jnp.dot(basis_rows, vector, precision=HIGH), ("row", "col")) / length
    once_clean = vector - jnp.dot(first_coef, basis_rows, precision=HIGH)
    second_coef, mean_square = lax.psum(
        (jnp.dot(basis_rows, once_clean, precision=HIGH), jnp.sum(once_clean * once_clean)),
        ("row", "col"),
    )
    second_coef = second_coef / length
    gram_coef = jnp.dot(gram_matrix, second_coef, precision=HIGH)
    mean_square = (
        mean_square / length
        - 2.0 * jnp.dot(second_coef, second_coef, precision=HIGH)
        + jnp.dot(second_coef, gram_coef, precision=HIGH)
    )
    twice_clean = once_clean - jnp.dot(second_coef, basis_rows, precision=HIGH)
    scale_now = jnp.sqrt(mean_square + 1e-06)
    cross_terms = (second_coef - gram_coef) / scale_now
    corner = mean_square / (scale_now * scale_now)
    upper_part = jnp.concatenate([gram_matrix, cross_terms[:, None]], axis=1)
    bottom = jnp.concatenate([cross_terms, corner[None]])[None, :]
    grown = jnp.concatenate([upper_part, bottom], axis=0)
    return (twice_clean / scale_now, scale_now, grown)


def per_device(
    u_start, v_start, keep_u, keep_v, v_next, tile_blocks, tile_rows, tile_cols, tile_count
):
    row_total = lax.axis_size("row")
    col_total = lax.axis_size("col")
    u_here = u_start.shape[0]
    u_part = lax.dynamic_slice_in_dim(keep_u, lax.axis_index("col") * u_here, u_here, 0)
    u_kept = lax.psum_scatter(
        jnp.dot(u_part.T, u_start, precision=HIGH), "col", scatter_dimension=1, tiled=True
    )
    v_here = v_start.shape[0]
    v_part = lax.dynamic_slice_in_dim(keep_v, lax.axis_index("row") * v_here, v_here, 0)
    v_kept = lax.psum_scatter(
        jnp.dot(v_part.T, v_start, precision=HIGH), "row", scatter_dimension=1, tiled=True
    )
    u_length = u_kept.shape[1] * row_total * col_total
    v_length = v_kept.shape[1] * row_total * col_total
    gram_left, gram_right = lax.psum(
        (jnp.dot(u_kept, u_kept.T, precision=HIGH), jnp.dot(v_kept, v_kept.T, precision=HIGH)),
        ("row", "col"),
    )
    gram_left = gram_left / u_length
    gram_right = gram_right / v_length
    tile_size = tile_blocks.shape[1]
    slot_total = tile_blocks.shape[0]
    row_blocks = u_kept.shape[1] * col_total // tile_size
    col_blocks = v_kept.shape[1] * row_total // tile_size
    active = (jnp.arange(slot_total, dtype=jnp.int32) < tile_count[0]).astype(jnp.float32)
    row_hot = (tile_rows[None, :] == jnp.arange(row_blocks, dtype=jnp.int32)[:, None]).astype(
        jnp.float32
    ) * active[None, :]
    col_hot = (tile_cols[None, :] == jnp.arange(col_blocks, dtype=jnp.int32)[:, None]).astype(
        jnp.float32
    ) * active[None, :]
    first_right, beta_start, gram_right = orthonormal(v_kept, v_next, v_length, gram_right)
    left_rows = u_kept
    right_rows = jnp.concatenate([v_kept, first_right[None, :]], axis=0)
    current = first_right
    alpha_list = []
    beta_list = []
    for iteration in range(STEPS):
        forward_gathered = lax.all_gather(current.astype(jnp.bfloat16), "row", axis=0, tiled=True)
        forward_picked = forward_gathered.reshape(col_blocks, tile_size)[tile_cols]
        forward_products = jnp.einsum(
            "tij,tj->ti", tile_blocks, forward_picked, preferred_element_type=jnp.float32
        )
        forward_partial_value = jnp.dot(row_hot, forward_products, precision=HIGH).reshape(-1)
        image = lax.psum_scatter(forward_partial_value, "col", scatter_dimension=0, tiled=True)
        left_new, alpha, gram_left = orthonormal(left_rows, image, u_length, gram_left)
        left_rows = jnp.concatenate([left_rows, left_new[None, :]], axis=0)
        gathered = lax.all_gather(left_new.astype(jnp.bfloat16), "col", axis=0, tiled=True)
        picked = gathered.reshape(row_blocks, tile_size)[tile_rows]
        products = jnp.einsum("tij,ti->tj", tile_blocks, picked, preferred_element_type=jnp.float32)
        partial_value = jnp.dot(col_hot, products, precision=HIGH).reshape(-1)
        back_image = lax.psum_scatter(partial_value, "row", scatter_dimension=0, tiled=True)
        current, beta, gram_right = orthonormal(right_rows, back_image, v_length, gram_right)
        right_rows = jnp.concatenate([right_rows, current[None, :]], axis=0)
        alpha_list.append(alpha)
        beta_list.append(beta)
    bidiagonal = jnp.stack([jnp.stack(alpha_list), jnp.stack(beta_list)])
    return (left_rows, right_rows, bidiagonal)


def solution(mesh):
    return jax.shard_map(
        per_device,
        mesh=mesh,
        in_specs=(
            P("col", "row"),
            P("row", "col"),
            P(),
            P(),
            P(("col", "row")),
            P(("row", "col"), None, None),
            P(("row", "col")),
            P(("row", "col")),
            P(("row", "col")),
        ),
        out_specs=(P(None, ("row", "col")), P(None, ("col", "row")), P()),
        check_vma=False,
    )
```

profile of v0, /device:TPU:0, one launch (start us, length us, event | category | flops | bytes accessed | tf_op | source)
XLA Modules:
  0.0 769.2 jit_solution(18316599006986476255)
XLA Ops:
  7.3 5.1 fusion.49
  12.5 4.5 fusion.51
  20.3 32.9 %reduce-scatter.5.cloned.1.call-done = f32[40,2048]{1,0:T(8,128)} async-done(((f32[40,16384]{1,0:T(8,128)}), f32[40,2048]{1,0:T(8,128)}) %reduce-scatter.5.cloned.1.call-update) | async-done | bytes 327696 | tf_op jit(solution)/shard_map/reduce_scatter | solution.py:48
  54.5 38.4 %psum.119 = f32[40]{0:T(128)S(1)} all-reduce(f32[40]{0:T(128)S(1)} %convolution_bitcast_fusion.18), channel_id=1, replica_groups=mesh['row'=8,'col'=4] {'row','col'}, use_global_device_ids=true, to_apply=%region_2.0 | all-reduce | flops 40 | bytes 320 | tf_op jit(solution)/shard_map/psum | solution.py:13
  96.0 1.6 fusion.128
  97.6 42.2 %all-reduce.8 = (f32[40]{0:T(128)S(1)}, f32[]{:T(128)}, f32[40,40]{1,0:T(8,128)S(1)}) all-reduce(f32[40]{0:T(128)S(1)} %convolution_bitcast_fusion.17, f32[]{:T(128)} %get-tuple-element.37, f32[40,40]{1,0:T(8,128)S(1)} %fusion.128), channel_id=1, replica_groups=mesh['row'=8,'col'=4] {'row','col'}, use_global_device_ids=true, to_apply=%region_3.0 | all-reduce | flops 1641 | bytes 13128 | tf_op jit(solution)/shard_map/psum | solution.py:15
  143.9 14.1 %all_gather.12 = bf16[16384]{0:T(1024)(128)(2,1)S(1)} all-gather(bf16[2048]{0:T(1024)(128)(2,1)S(1)} %get-tuple-element.35), channel_id=1, replica_groups=mesh['row'=8,'col'=4] {'row'}, dimensions={0}, use_global_device_ids=true | all-gather | bytes 36864 | tf_op jit(solution)/shard_map/all_gather | solution.py:77
  158.7 5.6 fusion.24
  165.5 1.9 fusion.129
  167.5 39.4 %all-reduce.14.cloned.1.call-done = f32[16384]{0:T(1024)} async-done(((f32[16384]{0:T(1024)}), f32[16384]{0:T(1024)}) %all-reduce.14.cloned.1.call-update) | async-done | bytes 65552
  207.6 1.7 convolution_bitcast_fusion.11
  209.3 39.4 %psum.123 = f32[40]{0:T(128)S(1)} all-reduce(f32[40]{0:T(128)S(1)} %convolution_bitcast_fusion.11), channel_id=1, replica_groups=mesh['row'=8,'col'=4] {'row','col'}, use_global_device_ids=true, to_apply=%region_8.0 | all-reduce | flops 40 | bytes 320 | tf_op jit(solution)/shard_map/psum | solution.py:13
  248.7 1.5 fusion.77
  251.5 1.7 convolution_bitcast_fusion.10
  253.2 41.4 %all-reduce.7 = (f32[40]{0:T(128)S(1)}, f32[]{:T(128)}, f32[40,40]{1,0:T(8,128)S(1)}) all-reduce(f32[40]{0:T(128)S(1)} %convolution_bitcast_fusion.10, f32[]{:T(128)} %get-tuple-element.33, f32[40,40]{1,0:T(8,128)S(1)} %fusion.129), channel_id=1, replica_groups=mesh['row'=8,'col'=4] {'row','col'}, use_global_device_ids=true, to_apply=%region_9.0 | all-reduce | flops 1641 | bytes 13128 | tf_op jit(solution)/shard_map/psum | solution.py:15
  297.4 1.5 fusion.75
  298.9 8.9 %all_gather.13 = bf16[16384]{0:T(1024)(128)(2,1)S(1)} all-gather(bf16[4096]{0:T(1024)(128)(2,1)S(1)} %get-tuple-element.31), channel_id=1, replica_groups=mesh['row'=8,'col'=4] {'col'}, dimensions={0}, use_global_device_ids=true | all-gather | bytes 40960 | tf_op jit(solution)/shard_map/all_gather | solution.py:86
  308.6 4.6 fusion.21
  314.4 53.6 %all-reduce.16.cloned.1.call-done = f32[16384]{0:T(1024)} async-done(((f32[16384]{0:T(1024)}), f32[16384]{0:T(1024)}) %all-reduce.16.cloned.1.call-update) | async-done | bytes 65552
  369.1 39.2 %psum.127 = f32[41]{0:T(128)S(1)} all-reduce(f32[41]{0:T(128)S(1)} %convolution_bitcast_fusion.16), channel_id=1, replica_groups=mesh['row'=8,'col'=4] {'row','col'}, use_global_device_ids=true, to_apply=%region_14.0 | all-reduce | flops 41 | bytes 328 | tf_op jit(solution)/shard_map/psum | solution.py:13
  410.3 40.0 %all-reduce.6 = (f32[41]{0:T(128)S(1)}, f32[]{:T(128)}) all-reduce(f32[41]{0:T(128)S(1)} %convolution_bitcast_fusion.15, f32[]{:T(128)} %get-tuple-element.29), channel_id=1, replica_groups=mesh['row'=8,'col'=4] {'row','col'}, use_global_device_ids=true, to_apply=%region_15.0 | all-reduce | flops 42 | bytes 336 | tf_op jit(solution)/shard_map/psum | solution.py:15
  453.5 14.1 %all_gather.14 = bf16[16384]{0:T(1024)(128)(2,1)S(1)} all-gather(bf16[2048]{0:T(1024)(128)(2,1)S(1)} %get-tuple-element.27), channel_id=1, replica_groups=mesh['row'=8,'col'=4] {'row'}, dimensions={0}, use_global_device_ids=true | all-gather | bytes 36864 | tf_op jit(solution)/shard_map/all_gather | solution.py:77
  468.4 5.6 fusion.18
  475.2 41.8 %all-reduce.18.cloned.1.call-done = f32[16384]{0:T(1024)} async-done(((f32[16384]{0:T(1024)}), f32[16384]{0:T(1024)}) %all-reduce.18.cloned.1.call-update) | async-done | bytes 65552
  518.4 39.2 %psum.130 = f32[41]{0:T(128)S(1)} all-reduce(f32[41]{0:T(128)S(1)} %convolution_bitcast_fusion.7), channel_id=1, replica_groups=mesh['row'=8,'col'=4] {'row','col'}, use_global_device_ids=true, to_apply=%region_19.0 | all-reduce | flops 41 | bytes 328 | tf_op jit(solution)/shard_map/psum | solution.py:13
  558.2 1.3 multiply_reduce_fusion
  560.2 41.4 %all-reduce.5 = (f32[41]{0:T(128)S(1)}, f32[]{:T(128)}) all-reduce(f32[41]{0:T(128)S(1)} %convolution_bitcast_fusion.6, f32[]{:T(128)} %get-tuple-element.25), channel_id=1, replica_groups=mesh['row'=8,'col'=4] {'row','col'}, use_global_device_ids=true, to_apply=%region_20.0 | all-reduce | flops 42 | bytes 336 | tf_op jit(solution)/shard_map/psum | solution.py:15
  605.6 9.1 %all_gather.15 = bf16[16384]{0:T(1024)(128)(2,1)S(1)} all-gather(bf16[4096]{0:T(1024)(128)(2,1)S(1)} %get-tuple-element.23), channel_id=1, replica_groups=mesh['row'=8,'col'=4] {'col'}, dimensions={0}, use_global_device_ids=true | all-gather | bytes 40960 | tf_op jit(solution)/shard_map/all_gather | solution.py:86
  615.4 4.6 fusion.15
  621.9 52.8 %all-reduce.20.cloned.1.call-done = f32[16384]{0:T(1024)} async-done(((f32[16384]{0:T(1024)}), f32[16384]{0:T(1024)}) %all-reduce.20.cloned.1.call-update) | async-done | bytes 65552
  675.8 39.3 %psum.133 = f32[42]{0:T(128)S(1)} all-reduce(f32[42]{0:T(128)S(1)} %convolution_bitcast_fusion.14), channel_id=1, replica_groups=mesh['row'=8,'col'=4] {'row','col'}, use_global_device_ids=true, to_apply=%region_24.0 | all-reduce | flops 42 | bytes 336 | tf_op jit(solution)/shard_map/psum | solution.py:13
  717.1 40.0 %all-reduce.4 = (f32[42]{0:T(128)S(1)}, f32[]{:T(128)}) all-reduce(f32[42]{0:T(128)S(1)} %convolution_bitcast_fusion.13, f32[]{:T(128)} %get-tuple-element.21), channel_id=1, replica_groups=mesh['row'=8,'col'=4] {'row','col'}, use_global_device_ids=true, to_apply=%region_25.0 | all-reduce | flops 43 | bytes 344 | tf_op jit(solution)/shard_map/psum | solution.py:15
  (104 shorter events, 34.0 us)
Async XLA Ops:
  7.2 5.3 copy-start
  7.2 10.6 %copy-start.7 = (u32[32]{0:T(128)S(1)}, u32[32]{0:T(128)}, u32[]{:S(2)}) copy-start(u32[32]{0:T(128)} %constant.69) | copy-start | bytes 388
  7.2 11.1 %copy-start.6 = (u32[32]{0:T(128)S(1)}, u32[32]{0:T(128)}, u32[]{:S(2)}) copy-start(u32[32]{0:T(128)} %constant.73) | copy-start | bytes 388
  7.2 13.0 %copy-start.5 = (s32[64]{0:T(128)S(1)}, s32[64]{0:T(128)}, u32[]{:S(2)}) copy-start(s32[64]{0:T(128)} %param.16) | copy-start | bytes 772
  7.2 13.1 %copy-start.4 = (s32[64]{0:T(128)S(1)}, s32[64]{0:T(128)}, u32[]{:S(2)}) copy-start(s32[64]{0:T(128)} %param.15) | copy-start | bytes 772
  7.2 46.0 %copy-start.3 = (f32[2048]{0:T(1024)S(1)}, f32[2048]{0:T(1024)}, u32[]{:S(2)}) copy-start(f32[2048]{0:T(1024)} %param.13) | copy-start | bytes 24580
  7.2 45.9 %reduce-scatter.5.cloned.1.call-start = ((), (), s32[]{:S(2)}) async-start(), calls=%async_computation.3 | async-start | bytes 2949120 | tf_op jit(solution)/shard_map/reduce_scatter | solution.py:48
  12.5 153.0 %reduce-scatter.3.cloned.1.call-start = ((), (), s32[]{:S(2)}) async-start(), calls=%async_computation.2 | async-start | bytes 3276800 | tf_op jit(solution)/shard_map/reduce_scatter | solution.py:43
  17.0 189.8 %all-reduce.14.cloned.1.call-start = ((), (), s32[]{:S(2)}) async-start(), calls=%async_computation.4 | async-start | bytes 131072
  165.4 202.6 %all-reduce.16.cloned.1.call-start = ((), (), s32[]{:S(2)}) async-start(), calls=%async_computation.5 | async-start | bytes 131072
  308.6 60.1 %copy-start.2 = (f32[40,2048]{1,0:T(8,128)S(1)}, f32[40,2048]{1,0:T(8,128)}, u32[]{:S(2)}) copy-start(f32[40,2048]{1,0:T(8,128)} %reduce-scatter.5.cloned.1.call-done) | copy-start | bytes 983044
  313.2 204.5 %copy-start.1 = (f32[40,4096]{1,0:T(8,128)S(1)}, f32[40,4096]{1,0:T(8,128)}, u32[]{:S(2)}) copy-start(f32[40,4096]{1,0:T(8,128)} %reduce-scatter.3.cloned.1.call-done) | copy-start | bytes 1966084
  314.1 202.9 %all-reduce.18.cloned.1.call-start = ((), (), s32[]{:S(2)}) async-start(), calls=%async_computation.6 | async-start | bytes 131072
  474.9 199.8 %all-reduce.20.cloned.1.call-start = ((), (), s32[]{:S(2)}) async-start(), calls=%async_computation.7 | async-start | bytes 131072
Sparse Core Ops, SparseCore 0:
  12.6 40.5 reduce-scatter.4
  56.2 39.4 reduce-scatter.2
  165.5 41.3 all-reduce.13
  314.2 53.6 all-reduce.15
  475.0 41.9 all-reduce.17
  621.0 53.6 all-reduce.19
where the time goes:
time: 772 us; the launch traced here: 769 us
  blocking collectives  447 us (58%)
  waiting for transfers between devices  221 us (29%)
  matrix products  55.3 us (7%)
  between operations  26.5 us (3%)
  other arithmetic  9.86 us (1%)
  local copies, waits for them, and re-layouts  9.85 us (1%)
    psum x5, blocking collectives, orthonormal(): lax.psum((jnp.dot(basis_rows, once_clean, precision=HIGH), jnp.sum(once_c...  205 us
    psum x5, blocking collectives, orthonormal(): lax.psum(jnp.dot(basis_rows, vector, precision=HIGH), ('row', 'col'))  196 us
    unnamed x10, waiting for transfers between devices  188 us
    reduce_scatter x1, waiting for transfers between devices, per_device(): lax.psum_scatter(jnp.dot(v_part.T, v_start, precision=HIGH), 'row', scatt...  32.9 us
    all_gather x2, blocking collectives, per_device(): lax.all_gather(current.astype(jnp.bfloat16), 'row', axis=0, tiled=True)  28.2 us
    all_gather x2, blocking collectives, per_device(): lax.all_gather(left_new.astype(jnp.bfloat16), 'col', axis=0, tiled=True)  18.1 us
  transfers between devices with their start and end apart: 6, of which 5 were waited for; matrix products, arithmetic and copies ran while one was open for 3% of the time, Pallas kernels for 0%

commit v1 on v0

v1 whole, which is shorter than its diff:
```python
import functools

import jax
import jax.numpy as jnp
from jax import lax
from jax.experimental import pallas as pl
from jax.experimental.pallas import tpu as pltpu
from jax.sharding import PartitionSpec as P

STEPS = 2
HIGH = lax.Precision.HIGHEST
F32 = jnp.float32
BF16 = jnp.bfloat16
LANE = 128
HALF = 64


def kernel(
    row_n, col_n, keep_n, u_hbm, v_hbm, keep_u, keep_v, v_next, tiles_hbm, rows_ref, cols_ref, count_ref,
    u_out, v_out, bi_out,
    u_all, v_all, tiles, u_rows, v_rows, u_vec, v_vec, big_col, big_row, sum_col, sum_row,
    v_gather, u_gather, u_parts, v_parts, u_recv, v_recv, picked, products,
    local_sem, init_u_send, init_u_recv, init_v_send, init_v_recv, send_sem,
    sum_col_sem, sum_row_sem, vg_sem, ug_sem, ur_sem, vr_sem,
):
    row_me = lax.axis_index("row")
    col_me = lax.axis_index("col")
    barrier = pltpu.get_barrier_semaphore()
    for k in range(1, row_n):
        pl.semaphore_signal(barrier, inc=1, device_id={"row": lax.rem(row_me + k, row_n)},
                            device_id_type=pl.DeviceIdType.MESH)
    for k in range(1, col_n):
        pl.semaphore_signal(barrier, inc=1, device_id={"col": lax.rem(col_me + k, col_n)},
                            device_id_type=pl.DeviceIdType.MESH)

    u_here, v_here = u_hbm.shape[0], v_hbm.shape[0]
    u_len, v_len = u_rows.shape[1], v_rows.shape[1]
    u_total = float(u_len * row_n * col_n)
    v_total = float(v_len * row_n * col_n)
    rows_p = u_rows.shape[0]
    keep_p = keep_u.shape[0]
    tile = tiles.shape[1]
    slots = tiles.shape[0]
    u_sub, v_sub = u_len // tile, v_len // tile

    def u_src(p):
        return u_hbm.at[:, pl.ds(pl.multiple_of(p * u_len, LANE), u_len)]

    def v_src(p):
        return v_hbm.at[:, pl.ds(pl.multiple_of(p * v_len, LANE), v_len)]

    u_dst = u_all.at[pl.ds(pl.multiple_of(col_me * u_here, 8), u_here), :]
    v_dst = v_all.at[pl.ds(pl.multiple_of(row_me * v_here, 8), v_here), :]
    own_v = pltpu.make_async_copy(v_src(row_me), v_dst, local_sem.at[0])
    own_u = pltpu.make_async_copy(u_src(col_me), u_dst, local_sem.at[1])
    own_t = pltpu.make_async_copy(tiles_hbm, tiles, local_sem.at[2])
    own_v.start()
    own_u.start()
    own_t.start()

    def send(axis, me, n, src, dst, sends, recvs):
        copies = []
        for k in range(1, n):
            target = lax.rem(me + k, n)
            copy = pltpu.make_async_remote_copy(
                src_ref=src(target, k), dst_ref=dst(k), send_sem=sends.at[k], recv_sem=recvs(k),
                device_id={axis: target}, device_id_type=pl.DeviceIdType.MESH)
            copy.start()
            copies.append(copy)
        return copies

    pl.semaphore_wait(barrier, row_n + col_n - 2)
    v_init = send("row", row_me, row_n, lambda p, k: v_src(p), lambda k: v_dst, init_v_send,
                  lambda k: init_v_recv.at[k])
    u_init = send("col", col_me, col_n, lambda p, k: u_src(p), lambda k: u_dst, init_u_send,
                  lambda k: init_u_recv.at[k])

    active = lax.broadcasted_iota(jnp.int32, (1, slots), 1) < count_ref[...]
    row_blocks = u_parts.shape[0] * u_sub
    col_blocks = v_parts.shape[0] * v_sub
    row_hot = jnp.where(
        (lax.broadcasted_iota(jnp.int32, (row_blocks, slots), 0) == rows_ref[...]) & active, 1.0, 0.0)
    col_hot = jnp.where(
        (lax.broadcasted_iota(jnp.int32, (col_blocks, slots), 0) == cols_ref[...]) & active, 1.0, 0.0)

    eye = (lax.broadcasted_iota(jnp.int32, (rows_p, LANE), 0)
           == lax.broadcasted_iota(jnp.int32, (rows_p, LANE), 1))
    row_id = lax.broadcasted_iota(jnp.int32, (rows_p, LANE), 0)
    lane_id = lax.broadcasted_iota(jnp.int32, (rows_p, LANE), 1)
    lane_row = lax.broadcasted_iota(jnp.int32, (1, LANE), 1)

    def to_row(column):
        return jnp.sum(jnp.where(eye, column, 0.0), axis=0, keepdims=True)

    def to_column(row):
        return jnp.sum(jnp.where(eye, row, 0.0), axis=1, keepdims=True)

    def all_sum(value, index, col_buf, row_buf):
        col_buf[col_me] = value
        for copy in send("col", col_me, col_n, lambda p, k: col_buf.at[col_me],
                         lambda k: col_buf.at[col_me], send_sem, lambda k: sum_col_sem.at[index, k]):
            copy.wait()
        total = col_buf[0]
        for i in range(1, col_n):
            total = total + col_buf[i]
        row_buf[row_me] = total
        for copy in send("row", row_me, row_n, lambda p, k: row_buf.at[row_me],
                         lambda k: row_buf.at[row_me], send_sem, lambda k: sum_row_sem.at[index, k]):
            copy.wait()
        total = row_buf[0]
        for i in range(1, row_n):
            total = total + row_buf[i]
        return total

    def small_sum(row, index):
        value = jnp.broadcast_to(row, (8, LANE))
        return all_sum(value, index, sum_col.at[index - 1], sum_row.at[index - 1])[0:1, :]

    def coef(basis, vec):
        acc = jnp.zeros((rows_p, LANE), F32)
        for j in range(vec.shape[1] // LANE):
            at = slice(j * LANE, (j + 1) * LANE)
            acc = acc + basis[:, at] * vec[:, at]
        return to_row(jnp.sum(acc, axis=1, keepdims=True))

    def remove(basis, vec, column):
        spread = jnp.broadcast_to(column, (rows_p, LANE))
        square = jnp.zeros((1, LANE), F32)
        for j in range(vec.shape[1] // LANE):
            at = slice(j * LANE, (j + 1) * LANE)
            new = vec[:, at] - jnp.sum(spread * basis[:, at], axis=0, keepdims=True)
            vec[:, at] = new
            square = square + new * new
        return jnp.sum(square, axis=1, keepdims=True)

    def orth(basis, vec, first_sum, index, length, gram, place):
        first = first_sum / length
        square = remove(basis, vec, to_column(first))
        sent = coef(basis, vec) + jnp.where(lane_row == LANE - 1, square, 0.0)
        got = small_sum(sent, index)
        square = jnp.sum(jnp.where(lane_row == LANE - 1, got, 0.0), axis=1, keepdims=True) / length
        second = jnp.where(lane_row < rows_p, got, 0.0) / length
        second_col = to_column(second)
        gram_coef = jnp.sum(gram * second_col, axis=0, keepdims=True)
        square = (square - 2.0 * jnp.sum(second * second, axis=1, keepdims=True)
                  + jnp.sum(second * gram_coef, axis=1, keepdims=True))
        remove(basis, vec, second_col)
        scale = jnp.sqrt(square + 1e-06)
        inverse = 1.0 / scale
        cross = (second - gram_coef) * inverse
        gram = jnp.where(row_id == place, cross, gram)
        gram = jnp.where(lane_id == place, to_column(cross), gram)
        gram = jnp.where((row_id == place) & (lane_id == place), square / (scale * scale), gram)
        new = vec[...] * inverse
        basis[place:place + 1, :] = new
        vec[...] = new
        return scale, gram

    def matvec(gathered, n, pick_hot, put_hot, contract):
        full = jnp.concatenate([gathered[i].astype(F32) for i in range(n)], axis=0).astype(BF16)
        picked[...] = lax.dot_general(pick_hot.astype(BF16), full, (((0,), (0,)), ((), ())),
                                      preferred_element_type=F32)
        sub = lax.broadcasted_iota(jnp.int32, (8, tile), 0)

        def group(g, carry):
            base = pl.multiple_of(g * 8, 8)
            left = picked[pl.ds(base, 8), :].astype(BF16)
            acc = jnp.zeros((8, tile), F32)
            for i in range(8):
                res = lax.dot_general(left, tiles[base + i], (((1,), (contract,)), ((), ())),
                                      preferred_element_type=F32)
                acc = jnp.where(sub == i, res, acc)
            products[pl.ds(base, 8), :] = acc
            return carry

        lax.fori_loop(0, slots // 8, group, 0)
        return jnp.dot(put_hot, products[...], precision=HIGH, preferred_element_type=F32)

    def gather(axis, me, n, vec, sub, buf, sems):
        own = jnp.concatenate([vec[:, i * tile:(i + 1) * tile] for i in range(sub)], axis=0)
        buf[me] = own.astype(BF16)
        for copy in send(axis, me, n, lambda p, k: buf.at[me], lambda k: buf.at[me], send_sem, sems):
            copy.wait()

    def scatter(axis, me, n, value, vec, sub, parts, recv, sems):
        for i in range(n):
            parts[i] = value[i * sub:(i + 1) * sub, :]
        for copy in send(axis, me, n, lambda p, k: parts.at[p], lambda k: recv.at[k], send_sem, sems):
            copy.wait()
        total = parts[me]
        for k in range(1, n):
            total = total + recv[k]
        for i in range(sub):
            vec[:, i * tile:(i + 1) * tile] = total[i:i + 1, :]

    u_rows[...] = jnp.zeros(u_rows.shape, F32)
    v_rows[...] = jnp.zeros(v_rows.shape, F32)
    v_vec[...] = v_next[...]
    own_v.wait()
    for copy in v_init:
        copy.wait()

    def kept(keep, source, target, length):
        for j in range(length // 512):
            at = slice(j * 512, (j + 1) * 512)
            target[0:keep_p, at] = jnp.dot(keep[...], source[:, at], precision=HIGH,
                                           preferred_element_type=F32)

    def half_gram(basis):
        small = basis[0:keep_p, :]
        wide = jnp.concatenate([basis[...], jnp.zeros((HALF - rows_p, basis.shape[1]), F32)], axis=0)
        return lax.dot_general(small, wide, (((1,), (1,)), ((), ())), precision=HIGH,
                               preferred_element_type=F32)

    kept(keep_v, v_all, v_rows, v_len)
    gram_v = half_gram(v_rows)
    first = coef(v_rows, v_vec)
    own_u.wait()
    for copy in u_init:
        copy.wait()
    kept(keep_u, u_all, u_rows, u_len)
    gram_u = half_gram(u_rows)
    payload = jnp.concatenate(
        [jnp.concatenate([gram_v, gram_u], axis=1), jnp.broadcast_to(first, (8, LANE))], axis=0)
    summed = all_sum(payload, 0, big_col, big_row)
    both = jnp.concatenate([summed[0:keep_p, :], jnp.zeros((rows_p - keep_p, LANE), F32)], axis=0)
    gram_v = jnp.where(lane_id < HALF, both, 0.0) / v_total
    gram_u = jnp.where(lane_id < HALF, pltpu.roll(both, HALF, 1), 0.0) / u_total

    scale, gram_v = orth(v_rows, v_vec, summed[keep_p:keep_p + 1, :], 1, v_total, gram_v, keep_n)
    own_t.wait()
    index = 2
    alphas, betas = [], []
    for step in range(STEPS):
        gather("row", row_me, row_n, v_vec, v_sub, v_gather.at[step], lambda k: vg_sem.at[step, k])
        partial = matvec(v_gather.at[step], row_n, col_hot, row_hot, 1)
        scatter("col", col_me, col_n, partial, u_vec, u_sub, u_parts, u_recv.at[step],
                lambda k: ur_sem.at[step, k])
        alpha, gram_u = orth(u_rows, u_vec, small_sum(coef(u_rows, u_vec), index), index + 1, u_total,
                             gram_u, keep_n + step)
        gather("col", col_me, col_n, u_vec, u_sub, u_gather.at[step], lambda k: ug_sem.at[step, k])
        partial = matvec(u_gather.at[step], col_n, row_hot, col_hot, 0)
        scatter("row", row_me, row_n, partial, v_vec, v_sub, v_parts, v_recv.at[step],
                lambda k: vr_sem.at[step, k])
        beta, gram_v = orth(v_rows, v_vec, small_sum(coef(v_rows, v_vec), index + 2), index + 3,
                            v_total, gram_v, keep_n + 1 + step)
        index += 4
        alphas.append(alpha)
        betas.append(beta)
    place_r = lax.broadcasted_iota(jnp.int32, (8, LANE), 0)
    place_l = lax.broadcasted_iota(jnp.int32, (8, LANE), 1)
    result = jnp.zeros((8, LANE), F32)
    for step in range(STEPS):
        result = jnp.where((place_r == 0) & (place_l == step), alphas[step], result)
        result = jnp.where((place_r == 1) & (place_l == step), betas[step], result)
    bi_out[...] = result
    u_out[...] = u_rows[0:u_out.shape[0], :]
    v_out[...] = v_rows[0:v_out.shape[0], :]


def per_device(
    u_start, v_start, keep_u, keep_v, v_next, tile_blocks, tile_rows, tile_cols, tile_count
):
    row_n = lax.axis_size("row")
    col_n = lax.axis_size("col")
    u_here, v_here = u_start.shape[0], v_start.shape[0]
    basis, keep_n = keep_u.shape
    u_len = u_start.shape[1] // col_n
    v_len = v_start.shape[1] // row_n
    slots, tile = tile_blocks.shape[0], tile_blocks.shape[1]
    rows_p = -(-(keep_n + 1 + STEPS) // 8) * 8
    keep_p = -(-keep_n // 8) * 8
    assert rows_p <= HALF
    pad = ((0, keep_p - keep_n), (0, 0))
    sums = 1 + 4 * STEPS
    dma = pltpu.SemaphoreType.DMA
    vmem = pl.BlockSpec(memory_space=pltpu.VMEM)
    hbm = pl.BlockSpec(memory_space=pl.ANY)
    u_sub, v_sub = u_len // tile, v_len // tile
    u_basis, v_basis, bidiagonal = pl.pallas_call(
        functools.partial(kernel, row_n, col_n, keep_n),
        out_shape=(
            jax.ShapeDtypeStruct((keep_n + STEPS, u_len), F32),
            jax.ShapeDtypeStruct((keep_n + 1 + STEPS, v_len), F32),
            jax.ShapeDtypeStruct((8, LANE), F32),
        ),
        in_specs=[hbm, hbm, vmem, vmem, vmem, hbm, vmem, vmem, vmem],
        out_specs=(vmem, vmem, vmem),
        scratch_shapes=[
            pltpu.VMEM((basis, u_len), F32),
            pltpu.VMEM((basis, v_len), F32),
            pltpu.VMEM(tile_blocks.shape, BF16),
            pltpu.VMEM((rows_p, u_len), F32),
            pltpu.VMEM((rows_p, v_len), F32),
            pltpu.VMEM((1, u_len), F32),
            pltpu.VMEM((1, v_len), F32),
            pltpu.VMEM((col_n, keep_p + 8, LANE), F32),
            pltpu.VMEM((row_n, keep_p + 8, LANE), F32),
            pltpu.VMEM((sums, col_n, 8, LANE), F32),
            pltpu.VMEM((sums, row_n, 8, LANE), F32),
            pltpu.VMEM((STEPS, row_n, v_sub, tile), BF16),
            pltpu.VMEM((STEPS, col_n, u_sub, tile), BF16),
            pltpu.VMEM((col_n, u_sub, tile), F32),
            pltpu.VMEM((row_n, v_sub, tile), F32),
            pltpu.VMEM((STEPS, col_n, u_sub, tile), F32),
            pltpu.VMEM((STEPS, row_n, v_sub, tile), F32),
            pltpu.VMEM((slots, tile), F32),
            pltpu.VMEM((slots, tile), F32),
            dma((3,)),
            dma((col_n,)),
            dma((col_n,)),
            dma((row_n,)),
            dma((row_n,)),
            dma((max(row_n, col_n),)),
            dma((sums + 1, col_n)),
            dma((sums + 1, row_n)),
            dma((STEPS, row_n)),
            dma((STEPS, col_n)),
            dma((STEPS, col_n)),
            dma((STEPS, row_n)),
        ],
        compiler_params=pltpu.CompilerParams(
            collective_id=0, has_side_effects=True, vmem_limit_bytes=48 * 1024 * 1024
        ),
    )(
        u_start, v_start, jnp.pad(keep_u.T, pad), jnp.pad(keep_v.T, pad), v_next.reshape(1, -1), tile_blocks,
        tile_rows.reshape(1, -1), tile_cols.reshape(1, -1), tile_count.reshape(1, 1),
    )
    return u_basis, v_basis, bidiagonal[:2, :STEPS]


def solution(mesh):
    return jax.shard_map(
        per_device,
        mesh=mesh,
        in_specs=(
            P("col", "row"),
            P("row", "col"),
            P(),
            P(),
            P(("col", "row")),
            P(("row", "col"), None, None),
            P(("row", "col")),
            P(("row", "col")),
            P(("row", "col")),
        ),
        out_specs=(P(None, ("row", "col")), P(None, ("col", "row")), P()),
        check_vma=False,
    )
```

time: 772 us -> 155 us (0.20)
  blocking collectives: 447 us -> 0 us
  waiting for transfers between devices: 221 us -> 0 us
  Pallas kernels: 0 us -> 145 us
  matrix products: 55.3 us -> 0 us
  between operations: 26.5 us -> 1.3 us
  other arithmetic: 9.86 us -> 0 us
    psum x10 -> x0, blocking collectives: 401 us -> none  [the longest x5 205 us: orthonormal(): lax.psum((jnp.dot(basis_rows, once_clean, precision=HIGH), jnp.sum(once_c...]
    unnamed x10 -> x0, waiting for transfers between devices: 188 us -> none
    pallas_call x0 -> x1, Pallas kernels: none -> 145 us  [per_device(): pl.pallas_call(functools.partial(kernel, row_n, col_n, keep_n), out_shape...]
    dot_general x37 -> x0, matrix products: 55.3 us -> none  [the longest x2 11.3 us: per_device(): jnp.einsum('tij,tj->ti', tile_blocks, forward_picked, preferred_element_t...]
    all_gather x4 -> x0, blocking collectives: 46.3 us -> none  [the longest x2 28.2 us: per_device(): lax.all_gather(current.astype(jnp.bfloat16), 'row', axis=0, tiled=True)]
    reduce_scatter x2 -> x0, waiting for transfers between devices: 32.9 us -> none  [the longest x1 32.9 us: per_device(): lax.psum_scatter(jnp.dot(v_part.T, v_start, precision=HIGH), 'row', scatt...]
  transfers between devices with their start and end apart: 6 -> 0, of which waited for: 5 -> 0; matrix products, arithmetic and copies ran while one was open for 3% -> 0% of each run, Pallas kernels for 0% -> 0%
where the time goes in v1:
time: 155 us
  Pallas kernels  145 us (94%)
  local copies, waits for them, and re-layouts  8.46 us (5%)
    pallas_call x1, Pallas kernels, per_device(): pl.pallas_call(functools.partial(kernel, row_n, col_n, keep_n), out_shape...  145 us
    unnamed x16, local copies, waits for them, and re-layouts  7.89 us

profile of v1, /device:TPU:0, one launch (start us, length us, event | category | flops | bytes accessed | tf_op | source)
XLA Modules:
  0.0 154.8 jit_solution(10028679483601556503)
XLA Ops:
  1.3 0.0 copy-start
  1.3 1.6 %copy-done = f32[32,16384]{1,0:T(8,128)S(1)} copy-done((f32[32,16384]{1,0:T(8,128)S(1)}, f32[32,16384]{1,0:T(8,128)}, u32[]{:S(2)}) %copy-start) | copy-done | bytes 2097176
  2.9 0.0 copy-start.1
  2.9 1.2 copy-done.1
  4.1 0.0 copy-start.2
  4.1 0.7 copy-done.2
  4.8 0.0 copy-start.3
  4.8 0.7 copy-done.3
  5.6 0.0 copy-start.4
  5.6 0.7 copy-done.4
  6.3 0.0 copy-start.5
  6.3 0.7 copy-done.5
  6.9 0.0 copy-start.6
  6.9 0.7 copy-done.6
  7.6 145.1 %shard_map.112 = (f32[42,4096]{1,0:T(8,128)S(1)}, f32[43,2048]{1,0:T(8,128)S(1)}, f32[8,128]{1,0:T(8,128)S(1)}) custom-call(f32[32,16384]{1,0:T(8,128)S(1)} %copy-done, f32[16,16384]{1,0:T(8,128)S(1)} %copy-done.1, f32[40,128]{1,0:T(8,128)S(1)} %bitcast.7, f32[40,128]{1,0:T(8,128)S(1)} %bitcast.8, f32[1,2048]{1,0:T(1,128)S(1)} %bitcast.9, ...), custom_call_target="tpu_custom_call" | custom-call | tf_op jit(solution)/shard_map/pallas_call | solution.py:280
  152.6 0.6 slice.3
  153.2 0.9 copy.15
  154.1 0.7 copy.16
Async XLA Ops:
  1.3 1.6 %copy-start = (f32[32,16384]{1,0:T(8,128)S(1)}, f32[32,16384]{1,0:T(8,128)}, u32[]{:S(2)}) copy-start(f32[32,16384]{1,0:T(8,128)} %u_hbm.1) | copy-start | bytes 6291460
  2.9 1.2 copy-start.1
  4.1 0.7 copy-start.2
  4.8 0.7 copy-start.3
  5.6 0.7 copy-start.4
  6.3 0.7 copy-start.5
  6.9 0.7 copy-start.6

commit v2 on v1

--- a/solution.py
+++ b/solution.py
@@ -13,25 +13,27 @@
 BF16 = jnp.bfloat16
 LANE = 128
 HALF = 64
+DIRECT = 32
 
 
 def kernel(
     row_n, col_n, keep_n, u_hbm, v_hbm, keep_u, keep_v, v_next, tiles_hbm, rows_ref, cols_ref, count_ref,
     u_out, v_out, bi_out,
-    u_all, v_all, tiles, u_rows, v_rows, u_vec, v_vec, big_col, big_row, sum_col, sum_row,
+    u_all, v_all, tiles, u_rows, v_rows, u_vec, v_vec, big_col, big_row, sum_col, sum_row, sum_all,
     v_gather, u_gather, u_parts, v_parts, u_recv, v_recv, picked, products,
     local_sem, init_u_send, init_u_recv, init_v_send, init_v_recv, send_sem,
-    sum_col_sem, sum_row_sem, vg_sem, ug_sem, ur_sem, vr_sem,
+    sum_col_sem, sum_row_sem, sum_all_sem, big_col_send, big_col_sem, big_row_send, big_row_sem,
+    vg_sem, ug_sem, ur_sem, vr_sem,
 ):
     row_me = lax.axis_index("row")
     col_me = lax.axis_index("col")
     barrier = pltpu.get_barrier_semaphore()
-    for k in range(1, row_n):
-        pl.semaphore_signal(barrier, inc=1, device_id={"row": lax.rem(row_me + k, row_n)},
-                            device_id_type=pl.DeviceIdType.MESH)
-    for k in range(1, col_n):
-        pl.semaphore_signal(barrier, inc=1, device_id={"col": lax.rem(col_me + k, col_n)},
-                            device_id_type=pl.DeviceIdType.MESH)
+    direct = row_n * col_n <= DIRECT
+    peers = [(a, b) for a in range(row_n) for b in range(col_n)
+             if (a or b) and (direct or not (a and b))]
+    for a, b in peers:
+        where = {"row": lax.rem(row_me + a, row_n), "col": lax.rem(col_me + b, col_n)}
+        pl.semaphore_signal(barrier, inc=1, device_id=where, device_id_type=pl.DeviceIdType.MESH)
 
     u_here, v_here = u_hbm.shape[0], v_hbm.shape[0]
     u_len, v_len = u_rows.shape[1], v_rows.shape[1]
@@ -69,7 +71,7 @@
             copies.append(copy)
         return copies
 
-    pl.semaphore_wait(barrier, row_n + col_n - 2)
+    pl.semaphore_wait(barrier, len(peers))
     v_init = send("row", row_me, row_n, lambda p, k: v_src(p), lambda k: v_dst, init_v_send,
                   lambda k: init_v_recv.at[k])
     u_init = send("col", col_me, col_n, lambda p, k: u_src(p), lambda k: u_dst, init_u_send,
@@ -95,26 +97,50 @@
     def to_column(row):
         return jnp.sum(jnp.where(eye, row, 0.0), axis=1, keepdims=True)
 
-    def all_sum(value, index, col_buf, row_buf):
-        col_buf[col_me] = value
-        for copy in send("col", col_me, col_n, lambda p, k: col_buf.at[col_me],
-                         lambda k: col_buf.at[col_me], send_sem, lambda k: sum_col_sem.at[index, k]):
-            copy.wait()
-        total = col_buf[0]
-        for i in range(1, col_n):
-            total = total + col_buf[i]
-        row_buf[row_me] = total
-        for copy in send("row", row_me, row_n, lambda p, k: row_buf.at[row_me],
-                         lambda k: row_buf.at[row_me], send_sem, lambda k: sum_row_sem.at[index, k]):
-            copy.wait()
-        total = row_buf[0]
-        for i in range(1, row_n):
-            total = total + row_buf[i]
-        return total
-
-    def small_sum(row, index):
-        value = jnp.broadcast_to(row, (8, LANE))
-        return all_sum(value, index, sum_col.at[index - 1], sum_row.at[index - 1])[0:1, :]
+    def add_up(buf, n):
+        parts = [buf[i] for i in range(n)]
+        while len(parts) > 1:
+            parts = [parts[i] + parts[i + 1] if i + 1 < len(parts) else parts[i]
+                     for i in range(0, len(parts), 2)]
+        return parts[0]
+
+    def col_start(buf, value, sends, recvs):
+        buf[col_me] = value
+        return send("col", col_me, col_n, lambda p, k: buf.at[col_me], lambda k: buf.at[col_me],
+                    sends, recvs)
+
+    def row_start(buf, value, sends, recvs):
+        buf[row_me] = value
+        return send("row", row_me, row_n, lambda p, k: buf.at[row_me], lambda k: buf.at[row_me],
+                    sends, recvs)
+
+    def sum_start(row, index):
+        if not direct:
+            return col_start(sum_col.at[index], row, send_sem, lambda k: sum_col_sem.at[index, k])
+        me = row_me * col_n + col_me
+        buf = sum_all.at[index]
+        buf[me] = row
+        copies = []
+        for k, (a, b) in enumerate(peers):
+            where = {"row": lax.rem(row_me + a, row_n), "col": lax.rem(col_me + b, col_n)}
+            copy = pltpu.make_async_remote_copy(
+                src_ref=buf.at[me], dst_ref=buf.at[me], send_sem=send_sem.at[k],
+                recv_sem=sum_all_sem.at[index, k], device_id=where,
+                device_id_type=pl.DeviceIdType.MESH)
+            copy.start()
+            copies.append(copy)
+        return copies
+
+    def sum_finish(copies, index):
+        for copy in copies:
+            copy.wait()
+        if direct:
+            return add_up(sum_all.at[index], row_n * col_n)
+        buf = sum_row.at[index]
+        for copy in row_start(buf, add_up(sum_col.at[index], col_n), send_sem,
+                              lambda k: sum_row_sem.at[index, k]):
+            copy.wait()
+        return add_up(buf, row_n)
 
     def coef(basis, vec):
         acc = jnp.zeros((rows_p, LANE), F32)
@@ -133,28 +159,33 @@
             square = square + new * new
         return jnp.sum(square, axis=1, keepdims=True)
 
-    def orth(basis, vec, first_sum, index, length, gram, place):
+    def orth(basis, vec, first_sum, index, length, gram_now, place, between=lambda: None):
         first = first_sum / length
         square = remove(basis, vec, to_column(first))
-        sent = coef(basis, vec) + jnp.where(lane_row == LANE - 1, square, 0.0)
-        got = small_sum(sent, index)
+        copies = sum_start(coef(basis, vec) + jnp.where(lane_row == LANE - 1, square, 0.0), index)
+        between()
+        got = sum_finish(copies, index)
         square = jnp.sum(jnp.where(lane_row == LANE - 1, got, 0.0), axis=1, keepdims=True) / length
         second = jnp.where(lane_row < rows_p, got, 0.0) / length
         second_col = to_column(second)
+        remove(basis, vec, second_col)
+        gram = gram_now()
         gram_coef = jnp.sum(gram * second_col, axis=0, keepdims=True)
         square = (square - 2.0 * jnp.sum(second * second, axis=1, keepdims=True)
                   + jnp.sum(second * gram_coef, axis=1, keepdims=True))
-        remove(basis, vec, second_col)
         scale = jnp.sqrt(square + 1e-06)
         inverse = 1.0 / scale
-        cross = (second - gram_coef) * inverse
-        gram = jnp.where(row_id == place, cross, gram)
-        gram = jnp.where(lane_id == place, to_column(cross), gram)
-        gram = jnp.where((row_id == place) & (lane_id == place), square / (scale * scale), gram)
-        new = vec[...] * inverse
-        basis[place:place + 1, :] = new
-        vec[...] = new
-        return scale, gram
+        vec[...] = vec[...] * inverse
+
+        def grow():
+            basis[place:place + 1, :] = vec[...]
+            cross = (second - gram_coef) * inverse
+            grown = jnp.where(row_id == place, cross, gram)
+            grown = jnp.where(lane_id == place, to_column(cross), grown)
+            corner = (row_id == place) & (lane_id == place)
+            return jnp.where(corner, square / (scale * scale), grown)
+
+        return scale, grow
 
     def matvec(gathered, n, pick_hot, put_hot, contract):
         full = jnp.concatenate([gathered[i].astype(F32) for i in range(n)], axis=0).astype(BF16)
@@ -176,11 +207,14 @@
         lax.fori_loop(0, slots // 8, group, 0)
         return jnp.dot(put_hot, products[...], precision=HIGH, preferred_element_type=F32)
 
-    def gather(axis, me, n, vec, sub, buf, sems):
+    def gather(axis, me, n, vec, sub, buf, sems, grow):
         own = jnp.concatenate([vec[:, i * tile:(i + 1) * tile] for i in range(sub)], axis=0)
         buf[me] = own.astype(BF16)
-        for copy in send(axis, me, n, lambda p, k: buf.at[me], lambda k: buf.at[me], send_sem, sems):
-            copy.wait()
+        copies = send(axis, me, n, lambda p, k: buf.at[me], lambda k: buf.at[me], send_sem, sems)
+        gram = grow()
+        for copy in copies:
+            copy.wait()
+        return gram
 
     def scatter(axis, me, n, value, vec, sub, parts, recv, sems):
         for i in range(n):
@@ -213,40 +247,55 @@
                                preferred_element_type=F32)
 
     kept(keep_v, v_all, v_rows, v_len)
-    gram_v = half_gram(v_rows)
-    first = coef(v_rows, v_vec)
+    first_copies = sum_start(coef(v_rows, v_vec), 0)
     own_u.wait()
     for copy in u_init:
         copy.wait()
     kept(keep_u, u_all, u_rows, u_len)
-    gram_u = half_gram(u_rows)
-    payload = jnp.concatenate(
-        [jnp.concatenate([gram_v, gram_u], axis=1), jnp.broadcast_to(first, (8, LANE))], axis=0)
-    summed = all_sum(payload, 0, big_col, big_row)
-    both = jnp.concatenate([summed[0:keep_p, :], jnp.zeros((rows_p - keep_p, LANE), F32)], axis=0)
-    gram_v = jnp.where(lane_id < HALF, both, 0.0) / v_total
-    gram_u = jnp.where(lane_id < HALF, pltpu.roll(both, HALF, 1), 0.0) / u_total
-
-    scale, gram_v = orth(v_rows, v_vec, summed[keep_p:keep_p + 1, :], 1, v_total, gram_v, keep_n)
-    own_t.wait()
+    both = jnp.concatenate([half_gram(v_rows), half_gram(u_rows)], axis=1)
+    gram_copies = col_start(big_col, both, big_col_send, lambda k: big_col_sem.at[k])
+
+    def gram_step():
+        for copy in gram_copies:
+            copy.wait()
+        gram_copies[:] = row_start(big_row, add_up(big_col, col_n), big_row_send,
+                                   lambda k: big_row_sem.at[k])
+
+    def gram_end():
+        for copy in gram_copies:
+            copy.wait()
+        total = add_up(big_row, row_n)
+        total = jnp.concatenate([total, jnp.zeros((rows_p - keep_p, LANE), F32)], axis=0)
+        grams.append(jnp.where(lane_id < HALF, pltpu.roll(total, HALF, 1), 0.0) / u_total)
+        return jnp.where(lane_id < HALF, total, 0.0) / v_total
+
+    grams = []
+    scale, grow = orth(v_rows, v_vec, sum_finish(first_copies, 0), 1, v_total, gram_end, keep_n,
+                       gram_step)
+    gram_u = grams[0]
     index = 2
     alphas, betas = [], []
     for step in range(STEPS):
-        gather("row", row_me, row_n, v_vec, v_sub, v_gather.at[step], lambda k: vg_sem.at[step, k])
+        gram_v = gather("row", row_me, row_n, v_vec, v_sub, v_gather.at[step],
+                        lambda k: vg_sem.at[step, k], grow)
+        if step == 0:
+            own_t.wait()
         partial = matvec(v_gather.at[step], row_n, col_hot, row_hot, 1)
         scatter("col", col_me, col_n, partial, u_vec, u_sub, u_parts, u_recv.at[step],
                 lambda k: ur_sem.at[step, k])
-        alpha, gram_u = orth(u_rows, u_vec, small_sum(coef(u_rows, u_vec), index), index + 1, u_total,
-                             gram_u, keep_n + step)
-        gather("col", col_me, col_n, u_vec, u_sub, u_gather.at[step], lambda k: ug_sem.at[step, k])
+        total = sum_finish(sum_start(coef(u_rows, u_vec), index), index)
+        alpha, grow = orth(u_rows, u_vec, total, index + 1, u_total, lambda: gram_u, keep_n + step)
+        gram_u = gather("col", col_me, col_n, u_vec, u_sub, u_gather.at[step],
+                        lambda k: ug_sem.at[step, k], grow)
         partial = matvec(u_gather.at[step], col_n, row_hot, col_hot, 0)
         scatter("row", row_me, row_n, partial, v_vec, v_sub, v_parts, v_recv.at[step],
                 lambda k: vr_sem.at[step, k])
-        beta, gram_v = orth(v_rows, v_vec, small_sum(coef(v_rows, v_vec), index + 2), index + 3,
-                            v_total, gram_v, keep_n + 1 + step)
+        total = sum_finish(sum_start(coef(v_rows, v_vec), index + 2), index + 2)
+        beta, grow = orth(v_rows, v_vec, total, index + 3, v_total, lambda: gram_v, keep_n + 1 + step)
         index += 4
         alphas.append(alpha)
         betas.append(beta)
+    grow()
     place_r = lax.broadcasted_iota(jnp.int32, (8, LANE), 0)
     place_l = lax.broadcasted_iota(jnp.int32, (8, LANE), 1)
     result = jnp.zeros((8, LANE), F32)
@@ -272,7 +321,10 @@
     keep_p = -(-keep_n // 8) * 8
     assert rows_p <= HALF
     pad = ((0, keep_p - keep_n), (0, 0))
-    sums = 1 + 4 * STEPS
+    sums = 2 + 4 * STEPS
+    total_n = row_n * col_n
+    direct_n = total_n if total_n <= DIRECT else 1
+    staged = 1 if total_n <= DIRECT else sums
     dma = pltpu.SemaphoreType.DMA
     vmem = pl.BlockSpec(memory_space=pltpu.VMEM)
     hbm = pl.BlockSpec(memory_space=pl.ANY)
@@ -294,10 +346,11 @@
             pltpu.VMEM((rows_p, v_len), F32),
             pltpu.VMEM((1, u_len), F32),
             pltpu.VMEM((1, v_len), F32),
-            pltpu.VMEM((col_n, keep_p + 8, LANE), F32),
-            pltpu.VMEM((row_n, keep_p + 8, LANE), F32),
-            pltpu.VMEM((sums, col_n, 8, LANE), F32),
-            pltpu.VMEM((sums, row_n, 8, LANE), F32),
+            pltpu.VMEM((col_n, keep_p, LANE), F32),
+            pltpu.VMEM((row_n, keep_p, LANE), F32),
+            pltpu.VMEM((staged, col_n, 1, LANE), F32),
+            pltpu.VMEM((staged, row_n, 1, LANE), F32),
+            pltpu.VMEM((sums, direct_n, 1, LANE), F32),
             pltpu.VMEM((STEPS, row_n, v_sub, tile), BF16),
             pltpu.VMEM((STEPS, col_n, u_sub, tile), BF16),
             pltpu.VMEM((col_n, u_sub, tile), F32),
@@ -311,9 +364,14 @@
             dma((col_n,)),
             dma((row_n,)),
             dma((row_n,)),
-            dma((max(row_n, col_n),)),
-            dma((sums + 1, col_n)),
-            dma((sums + 1, row_n)),
+            dma((max(row_n, col_n, direct_n),)),
+            dma((staged, col_n)),
+            dma((staged, row_n)),
+            dma((sums, direct_n)),
+            dma((col_n,)),
+            dma((col_n,)),
+            dma((row_n,)),
+            dma((row_n,)),
             dma((STEPS, row_n)),
             dma((STEPS, col_n)),
             dma((STEPS, col_n)),

time: 155 us -> 134 us (0.86)
  Pallas kernels: 145 us -> 123 us
    pallas_call x1, Pallas kernels: 145 us -> 123 us  [per_device(): pl.pallas_call(functools.partial(kernel, row_n, col_n, keep_n), out_shape...]
where the time goes in v2:
time: 134 us; the launch traced here: 133 us
  Pallas kernels  123 us (92%)
  local copies, waits for them, and re-layouts  8.46 us (6%)
    pallas_call x1, Pallas kernels, per_device(): pl.pallas_call(functools.partial(kernel, row_n, col_n, keep_n), out_shape...  123 us
    unnamed x16, local copies, waits for them, and re-layouts  7.89 us

profile of v2, /device:TPU:0, one launch (start us, length us, event | category | flops | bytes accessed | tf_op | source)
XLA Modules:
  0.0 133.2 jit_solution(12603945513314967519)
XLA Ops:
  1.3 0.0 copy-start
  1.3 1.6 %copy-done = f32[32,16384]{1,0:T(8,128)S(1)} copy-done((f32[32,16384]{1,0:T(8,128)S(1)}, f32[32,16384]{1,0:T(8,128)}, u32[]{:S(2)}) %copy-start) | copy-done | bytes 2097176
  2.9 0.0 copy-start.1
  2.9 1.2 copy-done.1
  4.1 0.0 copy-start.2
  4.1 0.7 copy-done.2
  4.8 0.0 copy-start.3
  4.8 0.7 copy-done.3
  5.6 0.0 copy-start.4
  5.6 0.7 copy-done.4
  6.3 0.0 copy-start.5
  6.3 0.7 copy-done.5
  6.9 0.0 copy-start.6
  6.9 0.7 copy-done.6
  7.6 123.4 %shard_map.112 = (f32[42,4096]{1,0:T(8,128)S(1)}, f32[43,2048]{1,0:T(8,128)S(1)}, f32[8,128]{1,0:T(8,128)S(1)}) custom-call(f32[32,16384]{1,0:T(8,128)S(1)} %copy-done, f32[16,16384]{1,0:T(8,128)S(1)} %copy-done.1, f32[40,128]{1,0:T(8,128)S(1)} %bitcast.7, f32[40,128]{1,0:T(8,128)S(1)} %bitcast.8, f32[1,2048]{1,0:T(1,128)S(1)} %bitcast.9, ...), custom_call_target="tpu_custom_call" | custom-call | tf_op jit(solution)/shard_map/pallas_call | solution.py:332
  131.0 0.6 slice.3
  131.6 0.9 copy.15
  132.4 0.7 copy.16
Async XLA Ops:
  1.3 1.6 %copy-start = (f32[32,16384]{1,0:T(8,128)S(1)}, f32[32,16384]{1,0:T(8,128)}, u32[]{:S(2)}) copy-start(f32[32,16384]{1,0:T(8,128)} %u_hbm.1) | copy-start | bytes 6291460
  2.9 1.2 copy-start.1
  4.1 0.7 copy-start.2
  4.8 0.7 copy-start.3
  5.6 0.7 copy-start.4
  6.3 0.7 copy-start.5
  6.9 0.7 copy-start.6
